TPU v7x, 16 devices: a whole 2x2x2 slice. The times are simulated.
16 devices in a mesh: stage: 2 (over z), data: 8 (over y, x, core).
Axes of the slice: x: 2, y: 2, z: 2, core: 2. Of those that a mesh axis runs over, the one named last changes fastest.
Arguments:
- inputs: bfloat16 [32, 256, 2560], P('data')
- targets: bfloat16 [32, 256, 2560], P('data')
- w_up: bfloat16 [2, 2560, 10240], P('stage')
- w_down: bfloat16 [2, 10240, 2560], P('stage')
Outputs:
- output 1: float32 [], replicated
- output 2: float32 [2, 2560, 10240], P('stage', 'data')
- output 3: float32 [2, 10240, 2560], P('stage', None, 'data')
All inputs are finite; a program needn't handle non-finite values.
Results may differ from a plain program's by a relative error of at most 0.0029477.
Values are sent between devices in bfloat16 or wider.
A program may use at most 1 GiB of HBM per device.

v0:
```python
import jax
import jax.numpy as jnp
from jax import lax
from jax.sharding import PartitionSpec as P, NamedSharding

CONTRACT_ROWS = (((0,), (0,)), ((), ()))
CONTRACT_COLS = (((1,), (1,)), ((), ()))


def layer_forward(h_in, w_up, w_down):
    pre_act = jnp.dot(h_in, w_up, preferred_element_type=jnp.float32)
    gelu_out = jax.nn.gelu(pre_act).astype(jnp.bfloat16)
    branch = jnp.dot(gelu_out, w_down, preferred_element_type=jnp.float32)
    return (h_in.astype(jnp.float32) + branch).astype(jnp.bfloat16)


def layer_backward(h_in, grad_out, w_up, w_down):
    pre_act = jnp.dot(h_in, w_up, preferred_element_type=jnp.float32)
    gelu_full, gelu_vjp = jax.vjp(jax.nn.gelu, pre_act)
    gelu_out = gelu_full.astype(jnp.bfloat16)
    g_down = lax.dot_general(gelu_out, grad_out, CONTRACT_ROWS, preferred_element_type=jnp.float32)
    grad_act = lax.dot_general(grad_out, w_down, CONTRACT_COLS, preferred_element_type=jnp.float32).astype(jnp.bfloat16)
    grad_pre = gelu_vjp(grad_act.astype(jnp.float32))[0].astype(jnp.bfloat16)
    g_up = lax.dot_general(h_in, grad_pre, CONTRACT_ROWS, preferred_element_type=jnp.float32)
    back_prod = lax.dot_general(grad_pre, w_up, CONTRACT_COLS, preferred_element_type=jnp.float32)
    grad_in = (grad_out.astype(jnp.float32) + back_prod).astype(jnp.bfloat16)
    return grad_in, g_up, g_down


def solution(mesh):
    n_stage = mesh.shape['stage']
    n_data = mesh.shape['data']
    fwd_perm = [(k, k + 1) for k in range(n_stage - 1)]
    bwd_perm = [(k + 1, k) for k in range(n_stage - 1)]

    def per_device(inputs, targets, w_up, w_down):
        n_micro, n_tok, width = inputs.shape
        n_local = w_up.shape[0]
        stage_id = lax.axis_index('stage')
        is_first = stage_id == 0
        is_last = stage_id == n_stage - 1
        n_slots = min(n_micro, 2 * n_stage)
        inv_total = 1.0 / (n_data * n_micro * n_tok)

        def run_forward(h_first):
            layer_ins = []
            h_cur = h_first
            for layer_idx in range(n_local):
                layer_ins.append(h_cur)
                h_cur = layer_forward(h_cur, w_up[layer_idx], w_down[layer_idx])
            return h_cur, jnp.stack(layer_ins)

        def skip_forward(h_first):
            return jnp.zeros_like(h_first), jnp.zeros((n_local, n_tok, width), jnp.bfloat16)

        def run_backward(operands):
            grad_cur, saved_in, acc_up, acc_down = operands
            grads_up = []
            grads_down = []
            for layer_idx in reversed(range(n_local)):
                grad_cur, g_up, g_down = layer_backward(saved_in[layer_idx], grad_cur, w_up[layer_idx], w_down[layer_idx])
                grads_up.append(g_up)
                grads_down.append(g_down)
            return grad_cur, acc_up + jnp.stack(grads_up[::-1]), acc_down + jnp.stack(grads_down[::-1])

        def skip_backward(operands):
            return jnp.zeros_like(operands[0]), operands[2], operands[3]

        def tick(tick_idx, loop_state):
            recv_fwd, recv_bwd, last_grad, stash, acc_up, acc_down, loss_sum = loop_state
            fwd_mb = tick_idx - stage_id
            fwd_ok = (fwd_mb >= 0) & (fwd_mb < n_micro)
            fwd_row = jnp.clip(fwd_mb, 0, n_micro - 1)
            x_mb = lax.dynamic_index_in_dim(inputs, fwd_row, 0, keepdims=False)
            h_first = jnp.where(is_first, x_mb, recv_fwd)
            h_out, layer_ins = lax.cond(fwd_ok, run_forward, skip_forward, h_first)
            y_mb = lax.dynamic_index_in_dim(targets, fwd_row, 0, keepdims=False)
            resid_diff = h_out.astype(jnp.float32) - y_mb.astype(jnp.float32)
            loss_sum = loss_sum + jnp.where(fwd_ok & is_last, jnp.sum(resid_diff * resid_diff), 0.0)
            top_grad = (resid_diff * inv_total).astype(jnp.bfloat16)

            bwd_mb = tick_idx - (2 * n_stage - 1 - stage_id)
            bwd_ok = (bwd_mb >= 0) & (bwd_mb < n_micro)
            bwd_slot = jnp.where(bwd_ok, bwd_mb % n_slots, n_slots)
            saved_in = lax.dynamic_index_in_dim(stash, bwd_slot, 0, keepdims=False)
            grad_first = jnp.where(is_last, last_grad, recv_bwd)
            grad_out, acc_up, acc_down = lax.cond(bwd_ok, run_backward, skip_backward, (grad_first, saved_in, acc_up, acc_down))

            fwd_slot = jnp.where(fwd_ok, fwd_mb % n_slots, n_slots)
            stash = lax.dynamic_update_index_in_dim(stash, layer_ins, fwd_slot, 0)
            recv_fwd = lax.ppermute(h_out, 'stage', fwd_perm)
            recv_bwd = lax.ppermute(grad_out, 'stage', bwd_perm)
            return recv_fwd, recv_bwd, top_grad, stash, acc_up, acc_down, loss_sum

        zero_act = jnp.zeros((n_tok, width), jnp.bfloat16)
        init_state = (zero_act, zero_act, zero_act, jnp.zeros((n_slots + 1, n_local, n_tok, width), jnp.bfloat16), jnp.zeros(w_up.shape, jnp.float32), jnp.zeros(w_down.shape, jnp.float32), jnp.zeros((), jnp.float32))
        final_state = lax.fori_loop(0, n_micro + 2 * n_stage - 1, tick, init_state)
        grad_up = lax.psum_scatter(final_state[4], 'data', scatter_dimension=1, tiled=True)
        grad_down = lax.psum_scatter(final_state[5], 'data', scatter_dimension=2, tiled=True)
        loss_total = lax.psum(final_state[6], ('stage', 'data')) * (0.5 * inv_total)
        return loss_total, grad_up, grad_down

    return jax.shard_map(per_device, mesh=mesh, in_specs=(P('data', None, None), P('data', None, None), P('stage', None, None), P('stage', None, None)), out_specs=(P(), P('stage', 'data', None), P('stage', None, 'data')), check_vma=False)
```

profile of v0, /device:TPU:0, one launch (start us, length us, event | category | flops | bytes accessed | tf_op | source)
XLA Modules:
  0.0 2865.7 jit_solution(3359758550154667164)
XLA Ops:
  11.8 32.7 %broadcast_in_dim.25 = f32[1,10240,2560]{2,1,0:T(8,128)} broadcast(f32[]{:T(128)} %constant.174.clone.1), dimensions={} | broadcast | bytes 104857600 | tf_op jit(solution)/shard_map/broadcast_in_dim | solution.py:96
  44.5 32.6 %broadcast_in_dim.24 = f32[1,2560,10240]{2,1,0:T(8,128)} broadcast(f32[]{:T(128)} %constant.174.clone.1), dimensions={} | broadcast | bytes 104857600 | tf_op jit(solution)/shard_map/broadcast_in_dim | solution.py:96
  77.1 1674.8 %while.28 = (s32[]{:T(128)}, bf16[256,2560]{1,0:T(8,128)(2,1)}, bf16[256,2560]{1,0:T(8,128)(2,1)S(1)}, bf16[256,2560]{1,0:T(8,128)(2,1)}, bf16[5,1,256,2560]{3,2...) while((s32[]{:T(128)}, bf16[256,2560]{1,0:T(8,128)(2,1)}, ...), condition=%wide.region_6.7_spmd.clone, body=%wide.region_0.6_spmd.clone.sunk | while | flops 94121492480 | bytes 782501568 | solution.py:97
  77.1 53.1 %conditional.6 = (bf16[256,2560]{1,0:T(8,128)(2,1)}, f32[256,2560]{1,0:T(8,128)}, bf16[1,1,256,2560]{3,2,1,0:T(8,128)(2,1)}) conditional(s32[]{:T(128)} %convert_element_type.157, () %tuple.91, (pred[]{:T(512)}, bf16[4,256,2560]{2,1,0:T(8,128)(2,1)}, s32[]{:T(128)}, bf16[256,2560]{1,0:T(8,128)(2,1)}, bf16[1,2560,10240]{2,1,0:T(8,128)(2,1)}, ...), branch_computations={%region_1.1_spmd, %region_2.2_spmd} | conditional | flops 26871726080 | bytes 128451616 | solution.py:76
  167.0 53.1 %conditional.6 = (bf16[256,2560]{1,0:T(8,128)(2,1)}, f32[256,2560]{1,0:T(8,128)}, bf16[1,1,256,2560]{3,2,1,0:T(8,128)(2,1)}) conditional(s32[]{:T(128)} %convert_element_type.157, () %tuple.91, (pred[]{:T(512)}, bf16[4,256,2560]{2,1,0:T(8,128)(2,1)}, s32[]{:T(128)}, bf16[256,2560]{1,0:T(8,128)(2,1)}, bf16[1,2560,10240]{2,1,0:T(8,128)(2,1)}, ...), branch_computations={%region_1.1_spmd, %region_2.2_spmd} | conditional | flops 26871726080 | bytes 128451616 | solution.py:76
  257.1 53.1 %conditional.6 = (bf16[256,2560]{1,0:T(8,128)(2,1)}, f32[256,2560]{1,0:T(8,128)}, bf16[1,1,256,2560]{3,2,1,0:T(8,128)(2,1)}) conditional(s32[]{:T(128)} %convert_element_type.157, () %tuple.91, (pred[]{:T(512)}, bf16[4,256,2560]{2,1,0:T(8,128)(2,1)}, s32[]{:T(128)}, bf16[256,2560]{1,0:T(8,128)(2,1)}, bf16[1,2560,10240]{2,1,0:T(8,128)(2,1)}, ...), branch_computations={%region_1.1_spmd, %region_2.2_spmd} | conditional | flops 26871726080 | bytes 128451616 | solution.py:76
  339.7 235.2 %collective-permute-done.1 = bf16[256,2560]{1,0:T(8,128)(2,1)S(1)} collective-permute-done((bf16[256,2560]{1,0:T(8,128)(2,1)}, bf16[256,2560]{1,0:T(8,128)(2,1)S(1)}, u32[]{:S(2)}, u32[]{:S(2)}) %collective-permute-start.1) | collective-permute-done | bytes 1310752 | tf_op jit(solution)/shard_map/while/body/eval_jaxpr/ppermute | solution.py:92
  574.9 53.1 %conditional.6 = (bf16[256,2560]{1,0:T(8,128)(2,1)}, f32[256,2560]{1,0:T(8,128)}, bf16[1,1,256,2560]{3,2,1,0:T(8,128)(2,1)}) conditional(s32[]{:T(128)} %convert_element_type.157, () %tuple.91, (pred[]{:T(512)}, bf16[4,256,2560]{2,1,0:T(8,128)(2,1)}, s32[]{:T(128)}, bf16[256,2560]{1,0:T(8,128)(2,1)}, bf16[1,2560,10240]{2,1,0:T(8,128)(2,1)}, ...), branch_computations={%region_1.1_spmd, %region_2.2_spmd} | conditional | flops 26871726080 | bytes 128451616 | solution.py:76
  631.7 233.7 %conditional.7 = (bf16[256,2560]{1,0:T(8,128)(2,1)}, f32[1,2560,10240]{2,1,0:T(8,128)}, f32[1,10240,2560]{2,1,0:T(8,128)}) conditional(s32[]{:T(128)} %convert_element_type.158, (f32[1,2560,10240]{2,1,0:T(8,128)}, f32[1,10240,2560]{2,1,0:T(8,128)}) %tuple.93, (pred[]{:T(512)}, s32[]{:T(128)}, bf16[256,2560]{1,0:T(8,128)(2,1)S(1)}, ...), branch_computations={%region_3.3_spmd, %region_4.4_spmd.clone} | conditional | flops 67245834240 | bytes 635699328 | solution.py:87
  711.8 83.8 %bitcast_add_fusion = f32[1,10240,2560]{2,1,0:T(8,128)} fusion(f32[1,10240,2560]{2,1,0:T(8,128)} %get-tuple-element.663, bf16[256,2560]{1,0:T(8,128)(2,1)S(1)} %select_select_fusion, f32[256,10240]{1,0:T(8,128)} %fusion.39), kind=kOutput, calls=%fused_computation.24 | convolution fusion | flops 13471580160 | bytes 221511680 | tf_op jit(solution)/shard_map/while/body/eval_jaxpr/cond/branch_1_fun/dot_general | solution.py:21
  795.6 69.8 %bitcast_add_fusion.1 = f32[1,2560,10240]{2,1,0:T(8,128)} fusion(f32[1,2560,10240]{2,1,0:T(8,128)} %get-tuple-element.662, bf16[256,10240]{1,0:T(8,128)(2,1)} %fusion.48, bf16[5,1,256,2560]{3,2,1,0:T(8,128)(2,1)} %get-tuple-element.658, s32[]{:T(128)S(6)} %select_n.152), kind=kOutput, calls=%fused_computation.25 | convolution fusion | flops 13447987200 | bytes 216268800 | tf_op jit(solution)/shard_map/while/body/eval_jaxpr/cond/branch_1_fun/dot_general | solution.py:24
  900.0 52.6 %collective-permute-start = (bf16[256,2560]{1,0:T(8,128)(2,1)}, bf16[256,2560]{1,0:T(8,128)(2,1)}, u32[]{:S(2)}, u32[]{:S(2)}) collective-permute-start(bf16[256,2560]{1,0:T(8,128)(2,1)} %get-tuple-element.823), channel_id=1, source_target_pairs={{0,8},{1,9},{2,10},{3,11},{4,12},{5,13},{6,14},{7,15}} | collective-permute-start | bytes 3932168 | tf_op jit(solution)/shard_map/while/body/eval_jaxpr/ppermute | solution.py:91
  952.6 233.7 %conditional.7 = (bf16[256,2560]{1,0:T(8,128)(2,1)}, f32[1,2560,10240]{2,1,0:T(8,128)}, f32[1,10240,2560]{2,1,0:T(8,128)}) conditional(s32[]{:T(128)} %convert_element_type.158, (f32[1,2560,10240]{2,1,0:T(8,128)}, f32[1,10240,2560]{2,1,0:T(8,128)}) %tuple.93, (pred[]{:T(512)}, s32[]{:T(128)}, bf16[256,2560]{1,0:T(8,128)(2,1)S(1)}, ...), branch_computations={%region_3.3_spmd, %region_4.4_spmd.clone} | conditional | flops 67245834240 | bytes 635699328 | solution.py:87
  1032.7 83.8 %bitcast_add_fusion = f32[1,10240,2560]{2,1,0:T(8,128)} fusion(f32[1,10240,2560]{2,1,0:T(8,128)} %get-tuple-element.663, bf16[256,2560]{1,0:T(8,128)(2,1)S(1)} %select_select_fusion, f32[256,10240]{1,0:T(8,128)} %fusion.39), kind=kOutput, calls=%fused_computation.24 | convolution fusion | flops 13471580160 | bytes 221511680 | tf_op jit(solution)/shard_map/while/body/eval_jaxpr/cond/branch_1_fun/dot_general | solution.py:21
  1116.5 69.8 %bitcast_add_fusion.1 = f32[1,2560,10240]{2,1,0:T(8,128)} fusion(f32[1,2560,10240]{2,1,0:T(8,128)} %get-tuple-element.662, bf16[256,10240]{1,0:T(8,128)(2,1)} %fusion.48, bf16[5,1,256,2560]{3,2,1,0:T(8,128)(2,1)} %get-tuple-element.658, s32[]{:T(128)S(6)} %select_n.152), kind=kOutput, calls=%fused_computation.25 | convolution fusion | flops 13447987200 | bytes 216268800 | tf_op jit(solution)/shard_map/while/body/eval_jaxpr/cond/branch_1_fun/dot_general | solution.py:24
  1222.2 233.7 %conditional.7 = (bf16[256,2560]{1,0:T(8,128)(2,1)}, f32[1,2560,10240]{2,1,0:T(8,128)}, f32[1,10240,2560]{2,1,0:T(8,128)}) conditional(s32[]{:T(128)} %convert_element_type.158, (f32[1,2560,10240]{2,1,0:T(8,128)}, f32[1,10240,2560]{2,1,0:T(8,128)}) %tuple.93, (pred[]{:T(512)}, s32[]{:T(128)}, bf16[256,2560]{1,0:T(8,128)(2,1)S(1)}, ...), branch_computations={%region_3.3_spmd, %region_4.4_spmd.clone} | conditional | flops 67245834240 | bytes 635699328 | solution.py:87
  1302.3 83.8 %bitcast_add_fusion = f32[1,10240,2560]{2,1,0:T(8,128)} fusion(f32[1,10240,2560]{2,1,0:T(8,128)} %get-tuple-element.663, bf16[256,2560]{1,0:T(8,128)(2,1)S(1)} %select_select_fusion, f32[256,10240]{1,0:T(8,128)} %fusion.39), kind=kOutput, calls=%fused_computation.24 | convolution fusion | flops 13471580160 | bytes 221511680 | tf_op jit(solution)/shard_map/while/body/eval_jaxpr/cond/branch_1_fun/dot_general | solution.py:21
  1386.1 69.8 %bitcast_add_fusion.1 = f32[1,2560,10240]{2,1,0:T(8,128)} fusion(f32[1,2560,10240]{2,1,0:T(8,128)} %get-tuple-element.662, bf16[256,10240]{1,0:T(8,128)(2,1)} %fusion.48, bf16[5,1,256,2560]{3,2,1,0:T(8,128)(2,1)} %get-tuple-element.658, s32[]{:T(128)S(6)} %select_n.152), kind=kOutput, calls=%fused_computation.25 | convolution fusion | flops 13447987200 | bytes 216268800 | tf_op jit(solution)/shard_map/while/body/eval_jaxpr/cond/branch_1_fun/dot_general | solution.py:24
  1490.8 233.7 %conditional.7 = (bf16[256,2560]{1,0:T(8,128)(2,1)}, f32[1,2560,10240]{2,1,0:T(8,128)}, f32[1,10240,2560]{2,1,0:T(8,128)}) conditional(s32[]{:T(128)} %convert_element_type.158, (f32[1,2560,10240]{2,1,0:T(8,128)}, f32[1,10240,2560]{2,1,0:T(8,128)}) %tuple.93, (pred[]{:T(512)}, s32[]{:T(128)}, bf16[256,2560]{1,0:T(8,128)(2,1)S(1)}, ...), branch_computations={%region_3.3_spmd, %region_4.4_spmd.clone} | conditional | flops 67245834240 | bytes 635699328 | solution.py:87
  1570.9 83.8 %bitcast_add_fusion = f32[1,10240,2560]{2,1,0:T(8,128)} fusion(f32[1,10240,2560]{2,1,0:T(8,128)} %get-tuple-element.663, bf16[256,2560]{1,0:T(8,128)(2,1)S(1)} %select_select_fusion, f32[256,10240]{1,0:T(8,128)} %fusion.39), kind=kOutput, calls=%fused_computation.24 | convolution fusion | flops 13471580160 | bytes 221511680 | tf_op jit(solution)/shard_map/while/body/eval_jaxpr/cond/branch_1_fun/dot_general | solution.py:21
  1654.7 69.8 %bitcast_add_fusion.1 = f32[1,2560,10240]{2,1,0:T(8,128)} fusion(f32[1,2560,10240]{2,1,0:T(8,128)} %get-tuple-element.662, bf16[256,10240]{1,0:T(8,128)(2,1)} %fusion.48, bf16[5,1,256,2560]{3,2,1,0:T(8,128)(2,1)} %get-tuple-element.658, s32[]{:T(128)S(6)} %select_n.152), kind=kOutput, calls=%fused_computation.25 | convolution fusion | flops 13447987200 | bytes 216268800 | tf_op jit(solution)/shard_map/while/body/eval_jaxpr/cond/branch_1_fun/dot_general | solution.py:24
  1751.9 95.8 %copy.8 = f32[1,10240,2560]{1,2,0:T(8,128)} copy(f32[1,10240,2560]{2,1,0:T(8,128)} %get-tuple-element.588) | data formatting | bytes 209715200 | tf_op jit(solution)/shard_map/while | solution.py:97
  1879.8 422.1 %reduce-scatter.7.cloned.1.call-done = f32[1,32,102400]{2,1,0:T(8,128)} async-done(((f32[1,256,102400]{2,1,0:T(8,128)}), f32[1,32,102400]{2,1,0:T(8,128)}) %reduce-scatter.7.cloned.1.call-update) | async-done | bytes 13107216
  2301.9 555.8 %reduce-scatter.9.cloned.1.call-done = f32[1,32,102400]{2,1,0:T(8,128)} async-done(((f32[1,256,102400]{2,1,0:T(8,128)}), f32[1,32,102400]{2,1,0:T(8,128)}) %reduce-scatter.9.cloned.1.call-update) | async-done | bytes 13107216
  (95 shorter events, 819.5 us)
Async XLA Ops:
  7.2 2294.8 %reduce-scatter.7.cloned.1.call-start = ((), (), s32[]{:S(2)}) async-start(), calls=%async_computation.2 | async-start | bytes 117964800
  130.2 30.4 %collective-permute-start = (bf16[256,2560]{1,0:T(8,128)(2,1)}, bf16[256,2560]{1,0:T(8,128)(2,1)}, u32[]{:S(2)}, u32[]{:S(2)}) collective-permute-start(bf16[256,2560]{1,0:T(8,128)(2,1)} %get-tuple-element.823), channel_id=1, source_target_pairs={{0,8},{1,9},{2,10},{3,11},{4,12},{5,13},{6,14},{7,15}} | collective-permute-start | bytes 3932168 | tf_op jit(solution)/shard_map/while/body/eval_jaxpr/ppermute | solution.py:91
  133.7 33.3 %collective-permute-start.1 = (bf16[256,2560]{1,0:T(8,128)(2,1)}, bf16[256,2560]{1,0:T(8,128)(2,1)S(1)}, u32[]{:S(2)}, u32[]{:S(2)}) collective-permute-start(bf16[256,2560]{1,0:T(8,128)(2,1)} %get-tuple-element.824), channel_id=1, source_target_pairs={{8,0},{9,1},{10,2},{11,3},{12,4},{13,5},{14,6},{15,7}} | collective-permute-start | bytes 3932168 | tf_op jit(solution)/shard_map/while/body/eval_jaxpr/ppermute | solution.py:92
  220.1 30.7 %collective-permute-start = (bf16[256,2560]{1,0:T(8,128)(2,1)}, bf16[256,2560]{1,0:T(8,128)(2,1)}, u32[]{:S(2)}, u32[]{:S(2)}) collective-permute-start(bf16[256,2560]{1,0:T(8,128)(2,1)} %get-tuple-element.823), channel_id=1, source_target_pairs={{0,8},{1,9},{2,10},{3,11},{4,12},{5,13},{6,14},{7,15}} | collective-permute-start | bytes 3932168 | tf_op jit(solution)/shard_map/while/body/eval_jaxpr/ppermute | solution.py:91
  225.0 32.2 %collective-permute-start.1 = (bf16[256,2560]{1,0:T(8,128)(2,1)}, bf16[256,2560]{1,0:T(8,128)(2,1)S(1)}, u32[]{:S(2)}, u32[]{:S(2)}) collective-permute-start(bf16[256,2560]{1,0:T(8,128)(2,1)} %get-tuple-element.824), channel_id=1, source_target_pairs={{8,0},{9,1},{10,2},{11,3},{12,4},{13,5},{14,6},{15,7}} | collective-permute-start | bytes 3932168 | tf_op jit(solution)/shard_map/while/body/eval_jaxpr/ppermute | solution.py:92
  310.2 29.5 %collective-permute-start = (bf16[256,2560]{1,0:T(8,128)(2,1)}, bf16[256,2560]{1,0:T(8,128)(2,1)}, u32[]{:S(2)}, u32[]{:S(2)}) collective-permute-start(bf16[256,2560]{1,0:T(8,128)(2,1)} %get-tuple-element.823), channel_id=1, source_target_pairs={{0,8},{1,9},{2,10},{3,11},{4,12},{5,13},{6,14},{7,15}} | collective-permute-start | bytes 3932168 | tf_op jit(solution)/shard_map/while/body/eval_jaxpr/ppermute | solution.py:91
  315.1 259.9 %collective-permute-start.1 = (bf16[256,2560]{1,0:T(8,128)(2,1)}, bf16[256,2560]{1,0:T(8,128)(2,1)S(1)}, u32[]{:S(2)}, u32[]{:S(2)}) collective-permute-start(bf16[256,2560]{1,0:T(8,128)(2,1)} %get-tuple-element.824), channel_id=1, source_target_pairs={{8,0},{9,1},{10,2},{11,3},{12,4},{13,5},{14,6},{15,7}} | collective-permute-start | bytes 3932168 | tf_op jit(solution)/shard_map/while/body/eval_jaxpr/ppermute | solution.py:92
  628.0 246.3 %collective-permute-start = (bf16[256,2560]{1,0:T(8,128)(2,1)}, bf16[256,2560]{1,0:T(8,128)(2,1)}, u32[]{:S(2)}, u32[]{:S(2)}) collective-permute-start(bf16[256,2560]{1,0:T(8,128)(2,1)} %get-tuple-element.823), channel_id=1, source_target_pairs={{0,8},{1,9},{2,10},{3,11},{4,12},{5,13},{6,14},{7,15}} | collective-permute-start | bytes 3932168 | tf_op jit(solution)/shard_map/while/body/eval_jaxpr/ppermute | solution.py:91
  865.4 30.5 %collective-permute-start.1 = (bf16[256,2560]{1,0:T(8,128)(2,1)}, bf16[256,2560]{1,0:T(8,128)(2,1)S(1)}, u32[]{:S(2)}, u32[]{:S(2)}) collective-permute-start(bf16[256,2560]{1,0:T(8,128)(2,1)} %get-tuple-element.824), channel_id=1, source_target_pairs={{8,0},{9,1},{10,2},{11,3},{12,4},{13,5},{14,6},{15,7}} | collective-permute-start | bytes 3932168 | tf_op jit(solution)/shard_map/while/body/eval_jaxpr/ppermute | solution.py:92
  900.0 295.2 %collective-permute-start = (bf16[256,2560]{1,0:T(8,128)(2,1)}, bf16[256,2560]{1,0:T(8,128)(2,1)}, u32[]{:S(2)}, u32[]{:S(2)}) collective-permute-start(bf16[256,2560]{1,0:T(8,128)(2,1)} %get-tuple-element.823), channel_id=1, source_target_pairs={{0,8},{1,9},{2,10},{3,11},{4,12},{5,13},{6,14},{7,15}} | collective-permute-start | bytes 3932168 | tf_op jit(solution)/shard_map/while/body/eval_jaxpr/ppermute | solution.py:91
  1186.3 29.3 %collective-permute-start.1 = (bf16[256,2560]{1,0:T(8,128)(2,1)}, bf16[256,2560]{1,0:T(8,128)(2,1)S(1)}, u32[]{:S(2)}, u32[]{:S(2)}) collective-permute-start(bf16[256,2560]{1,0:T(8,128)(2,1)} %get-tuple-element.824), channel_id=1, source_target_pairs={{8,0},{9,1},{10,2},{11,3},{12,4},{13,5},{14,6},{15,7}} | collective-permute-start | bytes 3932168 | tf_op jit(solution)/shard_map/while/body/eval_jaxpr/ppermute | solution.py:92
  1219.7 245.0 %collective-permute-start = (bf16[256,2560]{1,0:T(8,128)(2,1)}, bf16[256,2560]{1,0:T(8,128)(2,1)}, u32[]{:S(2)}, u32[]{:S(2)}) collective-permute-start(bf16[256,2560]{1,0:T(8,128)(2,1)} %get-tuple-element.823), channel_id=1, source_target_pairs={{0,8},{1,9},{2,10},{3,11},{4,12},{5,13},{6,14},{7,15}} | collective-permute-start | bytes 3932168 | tf_op jit(solution)/shard_map/while/body/eval_jaxpr/ppermute | solution.py:91
  1455.9 28.3 collective-permute-start.1
  1488.3 245.1 %collective-permute-start = (bf16[256,2560]{1,0:T(8,128)(2,1)}, bf16[256,2560]{1,0:T(8,128)(2,1)}, u32[]{:S(2)}, u32[]{:S(2)}) collective-permute-start(bf16[256,2560]{1,0:T(8,128)(2,1)} %get-tuple-element.823), channel_id=1, source_target_pairs={{0,8},{1,9},{2,10},{3,11},{4,12},{5,13},{6,14},{7,15}} | collective-permute-start | bytes 3932168 | tf_op jit(solution)/shard_map/while/body/eval_jaxpr/ppermute | solution.py:91
  1724.5 27.3 collective-permute-start.1
  1751.9 1105.8 %reduce-scatter.9.cloned.1.call-start = ((), (), s32[]{:S(2)}) async-start(), calls=%async_computation.3 | async-start | bytes 117964800
Sparse Core Ops, SparseCore 0:
  1752.0 549.8 reduce-scatter.6
  2306.1 551.5 reduce-scatter.8
where the time goes:
time: 2870 us
  waiting for transfers between devices  1360 us (47%)
  matrix products  1130 us (39%)
  local copies, waits for them, and re-layouts  199 us (7%)
  starting transfers between devices  80.1 us (3%)
  other arithmetic  46.9 us (2%)
  blocking collectives  31.4 us (1%)
    unnamed x4, waiting for transfers between devices  978 us
    dot_general x4, matrix products, layer_backward(): lax.dot_general(gelu_out, grad_out, CONTRACT_ROWS, preferred_element_type...  335 us
    ppermute x7, waiting for transfers between devices, tick(): recv_bwd = lax.ppermute(grad_out, 'stage', bwd_perm)  328 us
    dot_general x4, matrix products, layer_backward(): lax.dot_general(h_in, grad_pre, CONTRACT_ROWS, preferred_element_type=jnp...  279 us
    dot_general x4, matrix products, layer_backward(): lax.dot_general(grad_out, w_down, CONTRACT_COLS, preferred_element_type=j...  110 us
    dot_general x4, matrix products, layer_backward(): pre_act = jnp.dot(h_in, w_up, preferred_element_type=jnp.float32)  106 us
    dot_general x4, matrix products, layer_forward(): branch = jnp.dot(gelu_out, w_down, preferred_element_type=jnp.float32)  102 us
    dot_general x4, matrix products, layer_forward(): pre_act = jnp.dot(h_in, w_up, preferred_element_type=jnp.float32)  100 us
  transfers between devices with their start and end apart: 16, of which 12 were waited for; matrix products, arithmetic and copies ran while one was open for 38% of the time, Pallas kernels for 0%

commit v1 on v0

v1 whole, which is shorter than its diff:
```python
import functools
import math

import jax
import jax.numpy as jnp
from jax import lax
from jax.experimental import pallas as pl
from jax.experimental.pallas import tpu as pltpu
from jax.sharding import PartitionSpec as P

F32 = jnp.float32
BF16 = jnp.bfloat16
MESH = pl.DeviceIdType.MESH
COLS = (((1,), (1,)), ((), ()))
GC = math.sqrt(2.0 / math.pi)


def dot(a, b):
    return jnp.dot(a, b, preferred_element_type=F32)


def dot_cols(a, b):
    return lax.dot_general(a, b, COLS, preferred_element_type=F32)


def gelu(u):
    return u * (0.5 * (1.0 + jnp.tanh(GC * (u + 0.044715 * (u * u * u)))))


def gelu_grad(u):
    u2 = u * u
    t = jnp.tanh(GC * (u + 0.044715 * (u2 * u)))
    return 0.5 * (1.0 + t) + (0.5 * u) * (1.0 - t * t) * (GC + (3.0 * 0.044715 * GC) * u2)


def loop(n, body):
    lax.fori_loop(0, n, lambda i, c: (body(i), c)[1], 0)


def kernel(dims, x, y, w1, w2, m1, r1, m2, r2, lb, hc, ec, hn, en, ub, gb, qb, vx, pb,
           wb1, wb2, lacc, wsem, z_s, z_r, d_s, d_r, v_s, v_r, n_s, n_r, ms_s, ms_r, pe_s, pe_r, ls_s, ls_r):
    nm, T, D, Fk, fs, inv = dims
    nj = Fk // fs
    nt = 2 * nm
    dq, dr = D // 4, D // 8
    s = lax.axis_index('stage')
    r = lax.axis_index('data')
    k = r % 2
    pr = r + 1 - 2 * k
    fx = r + 2 - 4 * ((r // 2) % 2)
    fy = r + 4 - 8 * (r // 4)
    nb = fy * (1 - k) + fx * k
    pe = fx * (1 - k) + fy * k
    fb = k * Fk
    own = pl.ds(pl.multiple_of(k * T, T), T)
    oth = pl.ds(pl.multiple_of((1 - k) * T, T), T)
    is0, is1 = s == 0, s == 1

    def fcols(j):
        return pl.ds(pl.multiple_of(j * fs, fs), fs)

    def remote(src, dst, ss, rs, dev):
        return pltpu.make_async_remote_copy(src_ref=src, dst_ref=dst, send_sem=ss, recv_sem=rs, device_id=dev, device_id_type=MESH)

    def sched(t):
        kind0, i0 = t // nm, t % nm
        mid = (t > 0) & (t < nt - 1)
        kind1 = jnp.where(mid, (t + 1) % 2, jnp.where(t == 0, 0, 1))
        i1 = jnp.where(mid, jnp.where(t % 2 == 1, (t + 1) // 2, (t - 2) // 2), jnp.where(t == 0, 0, nm - 1))
        return jnp.where(is1, kind1, kind0), jnp.where(is1, i1, i0)

    def weights(g):
        j, sl = g % nj, g % 2
        cols = pl.ds(pl.multiple_of(fb + j * fs, fs), fs)
        return (pltpu.make_async_copy(w1.at[:, cols], wb1.at[sl], wsem.at[0, sl]),
                pltpu.make_async_copy(w2.at[cols, :], wb2.at[sl], wsem.at[1, sl]))

    for c in weights(0):
        c.start()

    @pl.when(is0)
    def _():
        for i in range(nm):
            remote(x.at[i], hc.at[i, own], d_s.at[i], d_r.at[i], (s, pr)).start()

    def phase1(ab, acc, uo, ui, go, tmp, yb, ob, alsem, usem, isem, gsem, psem, lsem, hsem):
        lacc[...] = jnp.zeros_like(lacc)

        def prep_a(t):
            kind, i = sched(t)

            @pl.when(is1 & (kind == 0))
            def _():
                c = remote(hc.at[i, own], hc.at[i, own], z_s.at[i], z_r.at[i], (s, r))
                c.wait_recv()
                remote(hc.at[i, own], hc.at[i, own], d_s.at[i], d_r.at[i], (s, pr)).start()

            @pl.when(is0 & (kind == 1))
            def _():
                c = remote(ec.at[i, own], ec.at[i, own], z_s.at[nm + i], z_r.at[nm + i], (s, r))
                c.wait_recv()
                remote(ec.at[i, own], ec.at[i, own], d_s.at[nm + i], d_r.at[nm + i], (s, pr)).start()

        def prep_b(t):
            kind, i = sched(t)
            ap = t % 2
            for kk, X, XN in ((0, hc, hn), (1, ec, en)):
                @pl.when(kind == kk)
                def _():
                    n = kk * nm + i
                    remote(X.at[i, own], X.at[i, oth], d_s.at[n], d_r.at[n], (s, pr)).wait_recv()
                    if kk == 1:
                        @pl.when(is1)
                        def _():
                            pltpu.make_async_copy(ob.at[0], ec.at[i, own], lsem.at[i]).wait()
                    if kk == 0:
                        @pl.when(is0)
                        def _():
                            remote(x.at[i], XN.at[i, own], n_s.at[n, 0], n_r.at[n, 0], (s, nb)).start()
                            pltpu.make_async_copy(x.at[i], ab.at[ap, own], alsem.at[ap, 0]).start()

                    @pl.when(is1 if kk == 0 else (s >= 0))
                    def _():
                        remote(X.at[i, own], XN.at[i, own], n_s.at[n, 0], n_r.at[n, 0], (s, nb)).start()
                        pltpu.make_async_copy(X.at[i, own], ab.at[ap, own], alsem.at[ap, 0]).start()
                    remote(X.at[i, oth], XN.at[i, oth], n_s.at[n, 1], n_r.at[n, 1], (s, nb)).start()
                    pltpu.make_async_copy(X.at[i, oth], ab.at[ap, oth], alsem.at[ap, 1]).start()

        def exchange(t):
            kind, i = sched(t)
            n = kind * nm + i
            return remote(acc.at[t % 2, oth], vx.at[n], v_s.at[n], v_r.at[n], (s, pr))

        def wait_out(t):
            kind, i = sched(t)

            @pl.when(is0 | (kind == 1))
            def _():
                n = kind * nm + i
                remote(ob.at[0], ec.at[i, own], z_s.at[n], z_r.at[n], (1 - s, r)).wait_send()

            @pl.when(is1 & (kind == 0))
            def _():
                remote(ob.at[0], ec.at[i, own], d_s.at[nm + i], d_r.at[nm + i], (s, pr)).wait_send()

        def post(t):
            kind, i = sched(t)
            n = kind * nm + i
            ap = t % 2
            exchange(t).wait()
            ld = pltpu.make_async_copy(vx.at[n], tmp, psem.at[0])
            ld.start()
            ly = pltpu.make_async_copy(y.at[i], yb, psem.at[1])
            ly.start()

            @pl.when(t >= 2)
            def _():
                wait_out(t - 2)
            ld.wait()
            ly.wait()
            last = is1 & (kind == 0)
            rb = min(64, T)

            def rows(b):
                lo = pl.ds(pl.multiple_of(b * rb, rb), rb)
                mine = pl.ds(pl.multiple_of(k * T + b * rb, rb), rb)
                h = (ab[ap, mine, :].astype(F32) + (acc[ap, mine, :] + tmp[lo, :])).astype(BF16)

                @pl.when(last)
                def _():
                    d = h.astype(F32) - yb[lo, :].astype(F32)
                    ob[ap, lo, :] = (d * inv).astype(BF16)
                    sq = jnp.sum((d * d).reshape(rb // 8, 8, D), axis=0)
                    part = lacc[...]
                    for c in range(D // 128):
                        part = part + sq[:, c * 128:(c + 1) * 128]
                    lacc[...] = part

                @pl.when(jnp.logical_not(last))
                def _():
                    ob[ap, lo, :] = h
            loop(T // rb, rows)

            @pl.when(is0)
            def _():
                remote(ob.at[ap], hc.at[i, own], z_s.at[n], z_r.at[n], (1 - s, r)).start()

            @pl.when(is1 & (kind == 1))
            def _():
                remote(ob.at[ap], ec.at[i, own], z_s.at[n], z_r.at[n], (1 - s, r)).start()

            @pl.when(last)
            def _():
                remote(ob.at[ap], ec.at[i, own], d_s.at[nm + i], d_r.at[nm + i], (s, pr)).start()
                pltpu.make_async_copy(ob.at[ap], ec.at[i, own], lsem.at[i]).start()

        def slot(t):
            kind, i = sched(t)
            ap = t % 2
            fwd, bwd = kind == 0, kind == 1

            def u_in(j):
                sl = (t * nj + j) % 2
                return pltpu.make_async_copy(ub.at[i, :, fcols(j)], ui.at[sl], isem.at[sl])

            def u_out(j):
                sl = (t * nj + j) % 2
                return pltpu.make_async_copy(uo.at[sl], ub.at[i, :, fcols(j)], usem.at[sl])

            def g_out(j, dst):
                sl = (t * nj + j) % 2
                return pltpu.make_async_copy(go.at[sl], dst.at[i, :, fcols(j)], gsem.at[sl])

            @pl.when(is0 | (t == 0))
            def _():
                prep_a(t)
                prep_b(t)

            @pl.when(bwd)
            def _():
                u_in(0).start()
            acc[ap] = jnp.zeros((2 * T, D), F32)
            pltpu.make_async_copy(hc.at[i, own], ab.at[ap, own], alsem.at[ap, 0]).wait()
            pltpu.make_async_copy(hc.at[i, oth], ab.at[ap, oth], alsem.at[ap, 1]).wait()

            @pl.when(is0 & fwd)
            def _():
                pltpu.make_async_copy(ab.at[ap, own], hc.at[i, own], hsem).start()

            def step(j):
                g = t * nj + j
                sl = g % 2
                for c in weights(g):
                    c.wait()
                for c in weights(g + 1):
                    c.start()

                @pl.when(is1 & (t > 0) & (j == nj // 2))
                def _():
                    post(t - 1)

                @pl.when(is1 & (t < nt - 1) & (j == nj // 2 + 1))
                def _():
                    prep_a(t + 1)

                @pl.when(is1 & (t < nt - 1) & (j == nj - 1))
                def _():
                    prep_b(t + 1)

                @pl.when(j >= 2)
                def _():
                    g_out(j - 2, gb).wait()

                @pl.when(fwd)
                def _():
                    @pl.when(j >= 2)
                    def _():
                        u_out(j - 2).wait()
                    uo[sl] = dot(ab[ap], wb1[sl])
                    go[sl] = gelu(uo[sl]).astype(BF16)
                    u_out(j).start()
                    g_out(j, gb).start()
                    acc[ap] += dot(go[sl], wb2[sl])

                @pl.when(bwd)
                def _():
                    u_in(j).wait()

                    @pl.when(j + 1 < nj)
                    def _():
                        u_in(j + 1).start()
                    p = dot_cols(ab[ap], wb2[sl]).astype(BF16)
                    go[sl] = (p.astype(F32) * gelu_grad(ui[sl])).astype(BF16)
                    g_out(j, qb).start()

                    @pl.when(is1)
                    def _():
                        acc[ap] += dot_cols(go[sl], wb1[sl])
            loop(nj, step)

            for j in (nj - 2, nj - 1):
                g_out(j, gb).wait()

                @pl.when(fwd)
                def _():
                    u_out(j).wait()

            @pl.when(is0 & fwd)
            def _():
                pltpu.make_async_copy(ab.at[ap, own], hc.at[i, own], hsem).wait()

            @pl.when(is1 | fwd)
            def _():
                exchange(t).start()

            @pl.when((is0 & fwd) | (is1 & (t == nt - 1)))
            def _():
                post(t)
        loop(nt, slot)

        for t in (2, 1):
            @pl.when(is0)
            def _():
                wait_out(nm - t)

            @pl.when(is1)
            def _():
                wait_out(nt - t)

    pl.run_scoped(
        phase1,
        pltpu.VMEM((2, 2 * T, D), BF16), pltpu.VMEM((2, 2 * T, D), F32),
        pltpu.VMEM((2, 2 * T, fs), F32), pltpu.VMEM((2, 2 * T, fs), F32), pltpu.VMEM((2, 2 * T, fs), BF16),
        pltpu.VMEM((T, D), F32), pltpu.VMEM((T, D), BF16), pltpu.VMEM((2, T, D), BF16),
        pltpu.SemaphoreType.DMA((2, 2)), pltpu.SemaphoreType.DMA((2,)), pltpu.SemaphoreType.DMA((2,)),
        pltpu.SemaphoreType.DMA((2,)), pltpu.SemaphoreType.DMA((2,)), pltpu.SemaphoreType.DMA((nm,)),
        pltpu.SemaphoreType.DMA,
    )

    def loss_copy(d):
        return remote(lacc, lb.at[r], ls_s.at[d], ls_r.at[r], (d // 8, d % 8))

    def loss_self():
        return pltpu.make_async_copy(lacc, lb.at[r], ls_s.at[8 + r])

    @pl.when(is1)
    def _():
        def send(d):
            @pl.when(d != 8 + r)
            def _():
                loss_copy(d).start()
        loop(16, send)
        loss_self().start()

    def phase2(ht, et, gv, qv, a, b, o, tb, tsem, asem, gqsem, osem):
        own_cols = pl.ds(pl.multiple_of((r // 2) * dq, 128), dq)
        peer_cols = pl.ds(pl.multiple_of((pe // 2) * dq, 128), dq)

        for q, X, dst in ((0, hc, ht), (0, hn, ht), (1, ec, et), (1, en, et)):
            near = X is hc or X is ec

            def build(i):
                if not near:
                    for h, rows in ((0, own), (1, oth)):
                        n = q * nm + i
                        remote(X.at[i, rows], X.at[i, rows], n_s.at[n, h], n_r.at[n, h], (s, nb)).wait_recv()
                cs = [pltpu.make_async_copy(X.at[i, :, cols], tb.at[c], tsem.at[c]) for c, cols in enumerate((own_cols, peer_cols))]
                for c in cs:
                    c.start()
                at = pl.multiple_of((i if near else nm + i) * 2 * T, 2 * T)
                for c in range(2):
                    cs[c].wait()
                    dst[c * dq:(c + 1) * dq, pl.ds(at, 2 * T)] = tb[c].T
            loop(nm, build)

        def stream(v):
            i, sl = v % nm, v % 2
            return (pltpu.make_async_copy(hn.at[i], a.at[sl], asem.at[0, sl]),
                    pltpu.make_async_copy(en.at[i], b.at[sl], asem.at[1, sl]))

        def saved(j, i):
            rows = pl.ds(pl.multiple_of(i * 2 * T, 2 * T), 2 * T)
            return (pltpu.make_async_copy(gb.at[i, :, fcols(j)], gv.at[rows], gqsem.at[0, i]),
                    pltpu.make_async_copy(qb.at[i, :, fcols(j)], qv.at[rows], gqsem.at[1, i]))

        def kept(q, j, m):
            cols = pl.ds(pl.multiple_of(fb + j * fs, fs), fs)
            mine = pltpu.make_async_copy(o.at[q, m], (m1, m2)[q].at[:, cols], osem.at[q, m])
            rest = pltpu.make_async_copy(o.at[q, m], pb.at[q, j, m], osem.at[q, m])
            return mine, rest

        def sends(j):
            cols = pl.ds(pl.multiple_of(fb + j * fs, fs), fs)
            out = []
            for q in range(2):
                out.append(remote(pb.at[q, j, 1 - k], (m1, m2)[q].at[:, cols], ms_s.at[q, j], ms_r.at[q, j], (s, pr)))
                for c in range(2):
                    out.append(remote(pb.at[q, j, 2 + c], (r1, r2)[q].at[:, cols], pe_s.at[q, c, j], pe_r.at[q, k, j], (s, pe - k + c)))
            return out

        def ship(j):
            for q in range(2):
                loop(4, lambda m: kept(q, j, m)[1].wait())
            for c in sends(j):
                c.start()

        for c in stream(0):
            c.start()

        def part(j):
            g = nt * nj + j
            ws = g % 2
            loop(nm, lambda i: [c.start() for c in saved(j, i)])
            for c in weights(g):
                c.wait()

            @pl.when(j + 1 < nj)
            def _():
                for c in weights(g + 1):
                    c.start()

            @pl.when(j >= 1)
            def _():
                ship(j - 1)

            def again(i):
                v = j * nm + i
                sl = v % 2
                for c in stream(v):
                    c.wait()

                @pl.when(v + 1 < nj * nm)
                def _():
                    for c in stream(v + 1):
                        c.start()
                rows = pl.ds(pl.multiple_of((nm + i) * 2 * T, 2 * T), 2 * T)
                u = dot(a[sl], wb1[ws])
                gv[rows, :] = gelu(u).astype(BF16)
                p = dot_cols(b[sl], wb2[ws]).astype(BF16)
                qv[rows, :] = (p.astype(F32) * gelu_grad(u)).astype(BF16)
            loop(nm, again)
            loop(nm, lambda i: [c.wait() for c in saved(j, i)])

            def grads(m):
                rows = pl.ds(pl.multiple_of(m * dr, dr), dr)
                o[0, m] = dot(ht[rows, :], qv[...])
                o[1, m] = dot(et[rows, :], gv[...])
                for q in range(2):
                    mine, rest = kept(q, j, m)

                    @pl.when(m == k)
                    def _():
                        mine.start()

                    @pl.when(m != k)
                    def _():
                        rest.start()
            loop(4, grads)
        loop(nj, part)
        ship(nj - 1)

        def finish(j):
            for c in sends(j):
                c.wait_send()
            cols = pl.ds(pl.multiple_of(fb + j * fs, fs), fs)
            for q in range(2):
                remote(pb.at[q, j, 0], (m1, m2)[q].at[:, cols], ms_s.at[q, j], ms_r.at[q, j], (s, pr)).wait_recv()
                for c in range(2):
                    remote(pb.at[q, j, 0], (r1, r2)[q].at[:, cols], pe_s.at[q, c, j], pe_r.at[q, c, j], (s, pr)).wait_recv()
        loop(nj, finish)

    nr = 2 * nm * 2 * T
    pl.run_scoped(
        phase2,
        pltpu.VMEM((2 * dq, nr), BF16), pltpu.VMEM((2 * dq, nr), BF16),
        pltpu.VMEM((nr, fs), BF16), pltpu.VMEM((nr, fs), BF16),
        pltpu.VMEM((2, 2 * T, D), BF16), pltpu.VMEM((2, 2 * T, D), BF16),
        pltpu.VMEM((2, 4, dr, fs), F32), pltpu.VMEM((2, 2 * T, dq), BF16),
        pltpu.SemaphoreType.DMA((2,)), pltpu.SemaphoreType.DMA((2, 2)), pltpu.SemaphoreType.DMA((2, nm)), pltpu.SemaphoreType.DMA((2, 4)),
    )

    def settle(n):
        @pl.when(is0 | (n < nm))
        def _():
            remote(hc.at[0, own], hc.at[0, own], d_s.at[n], d_r.at[n], (s, pr)).wait_send()
        for h in range(2):
            remote(hc.at[0, own], hn.at[0, own], n_s.at[n, h], n_r.at[n, h], (s, nb)).wait_send()
    loop(nt, settle)

    @pl.when(is1)
    def _():
        def sent(d):
            @pl.when(d != 8 + r)
            def _():
                loss_copy(d).wait_send()
        loop(16, sent)
        loss_self().wait()

    def got(n):
        @pl.when(is0 | (n != r))
        def _():
            remote(lacc, lb.at[n], ls_s.at[n], ls_r.at[n], (s, r)).wait_recv()
    loop(8, got)


def solution(mesh):
    n_data = mesh.shape['data']

    def per_device(inputs, targets, w_up, w_down):
        nm, T, D = inputs.shape
        F = w_up.shape[2]
        Fk = F // 2
        fs = min(512, Fk // 2)
        nj = Fk // fs
        dr = D // 8
        inv = 1.0 / (n_data * nm * T)
        dims = (nm, T, D, Fk, fs, inv)
        sd = jax.ShapeDtypeStruct
        out_shape = [
            sd((dr, F), F32), sd((dr, F), F32), sd((dr, F), F32), sd((dr, F), F32), sd((8, 8, 128), F32),
            sd((nm, 2 * T, D), BF16), sd((nm, 2 * T, D), BF16), sd((nm, 2 * T, D), BF16), sd((nm, 2 * T, D), BF16),
            sd((nm, 2 * T, Fk), F32), sd((nm, 2 * T, Fk), BF16), sd((nm, 2 * T, Fk), BF16),
            sd((2 * nm, T, D), F32), sd((2, nj, 4, dr, fs), F32),
        ]
        any_spec = pl.BlockSpec(memory_space=pl.ANY)
        sem = pltpu.SemaphoreType.DMA
        units = 8 * 2 * nm * T * D * F
        outs = pl.pallas_call(
            functools.partial(kernel, dims),
            out_shape=out_shape,
            in_specs=[any_spec] * 4,
            out_specs=[any_spec] * len(out_shape),
            scratch_shapes=[
                pltpu.VMEM((2, D, fs), BF16), pltpu.VMEM((2, fs, D), BF16), pltpu.VMEM((8, 128), F32),
                sem((2, 2)), sem((2 * nm,)), sem((2 * nm,)), sem((2 * nm,)), sem((2 * nm,)), sem((2 * nm,)), sem((2 * nm,)),
                sem((2 * nm, 2)), sem((2 * nm, 2)), sem((2, nj)), sem((2, nj)), sem((2, 2, nj)), sem((2, 2, nj)), sem((16,)), sem((8,)),
            ],
            compiler_params=pltpu.CompilerParams(has_side_effects=True, vmem_limit_bytes=67_000_000),
            cost_estimate=pl.CostEstimate(flops=units, bytes_accessed=10**9, transcendentals=0),
            name='train_step',
        )(inputs, targets, w_up.reshape(D, F), w_down.reshape(F, D))
        m1, r1, m2, r2, lb = outs[:5]
        loss = jnp.sum(lb) * (0.5 * inv)
        return loss, (m1 + r1)[None], (m2 + r2).T[None]

    return jax.shard_map(per_device, mesh=mesh, in_specs=(P('data', None, None), P('data', None, None), P('stage', None, None), P('stage', None, None)), out_specs=(P(), P('stage', 'data', None), P('stage', None, 'data')), check_vma=False)
```

time: 2870 us -> 880 us (0.31)
  waiting for transfers between devices: 1360 us -> 0 us
  matrix products: 1130 us -> 0 us
  Pallas kernels: 0 us -> 847 us
  local copies, waits for them, and re-layouts: 199 us -> 0 us
  starting transfers between devices: 80.1 us -> 0 us
  blocking collectives: 31.4 us -> 0 us
    dot_general x28 -> x0, matrix products: 1130 us -> none  [the longest x4 335 us: layer_backward(): lax.dot_general(gelu_out, grad_out, CONTRACT_ROWS, preferred_element_type...]
    unnamed x4 -> x0, waiting for transfers between devices: 978 us -> none
    pallas_call x0 -> x1, Pallas kernels: none -> 847 us  [per_device(): pl.pallas_call(functools.partial(kernel, dims), out_shape=out_shape, in_s...]
    ppermute x14 -> x0, waiting for transfers between devices: 379 us -> none  [the longest x7 328 us: tick(): recv_bwd = lax.ppermute(grad_out, 'stage', bwd_perm)]
    while x1 -> x0, local copies, waits for them, and re-layouts: 95.8 us -> none  [per_device(): final_state = lax.fori_loop(0, n_micro + 2 * n_stage - 1, tick, init_state)]
    ppermute x14 -> x0, starting transfers between devices: 80.1 us -> none  [the longest x7 71.1 us: tick(): recv_fwd = lax.ppermute(h_out, 'stage', fwd_perm)]
    broadcast_in_dim x6 -> x0, local copies, waits for them, and re-layouts: 72.1 us -> none  [the longest x1 32.7 us: per_device(): jnp.zeros(w_down.shape, jnp.float32)]
    psum x1 -> x0, blocking collectives: 31.4 us -> none  [per_device(): loss_total = lax.psum(final_state[6], ('stage', 'data')) * (0.5 * inv_total)]
  transfers between devices with their start and end apart: 16 -> 0, of which waited for: 12 -> 0; matrix products, arithmetic and copies ran while one was open for 38% -> 0% of each run, Pallas kernels for 0% -> 0%
where the time goes in v1:
time: 880 us; the launch traced here: 878 us
  Pallas kernels  847 us (96%)
  other arithmetic  28.3 us (3%)
    pallas_call x1, Pallas kernels, per_device(): pl.pallas_call(functools.partial(kernel, dims), out_shape=out_shape, in_s...  847 us
    broadcast_in_dim x1, other arithmetic, per_device(): return (loss, (m1 + r1)[None], (m2 + r2).T[None])  27 us

profile of v1, /device:TPU:0, one launch (start us, length us, event | category | flops | bytes accessed | tf_op | source)
XLA Modules:
  0.0 877.6 jit_solution(7307100756164822856)
XLA Ops:
  0.6 846.8 %train_step.1 = (f32[320,10240]{1,0:T(8,128)}, f32[320,10240]{1,0:T(8,128)}, f32[320,10240]{1,0:T(8,128)}, f32[320,10240]{1,0:T(8,128)}, f32[8,8,128]{2,1,0:T(8,...) custom-call(bf16[4,256,2560]{2,1,0:T(8,128)(2,1)} %x.1, ...), custom_call_target="tpu_custom_call" | custom-call | flops 429496729600 | bytes 1000000000 | tf_op jit(solution)/shard_map/train_step/pallas_call | solution.py:508
  847.5 1.4 reduce_sum.9
  849.5 27.0 %add_bitcast_fusion = (f32[1,10240,320]{1,2,0:T(8,128)}, f32[1,320,10240]{2,1,0:T(8,128)}) fusion(f32[320,10240]{1,0:T(8,128)} %get-tuple-element.11, f32[320,10240]{1,0:T(8,128)} %get-tuple-element.12, f32[320,10240]{1,0:T(8,128)} %get-tuple-element.9, f32[320,10240]{1,0:T(8,128)} %get-tuple-element.10), kind=kLoop, calls=%fused_computation | loop fusion | flops 6553600 | bytes 78643200 | tf_op jit(solution)/shard_map/broadcast_in_dim | solution.py:524

commit v2 on v1

v2 whole, which is shorter than its diff:
```python
import functools
import math

import jax
import jax.numpy as jnp
from jax import lax
from jax.experimental import pallas as pl
from jax.experimental.pallas import tpu as pltpu
from jax.sharding import PartitionSpec as P

F32 = jnp.float32
BF16 = jnp.bfloat16
MESH = pl.DeviceIdType.MESH
COLS = (((1,), (1,)), ((), ()))
GC = math.sqrt(2.0 / math.pi)
DMA = pltpu.SemaphoreType.DMA
VMEM = pltpu.VMEM


def dot(a, b):
    return jnp.dot(a, b, preferred_element_type=F32)


def dot_cols(a, b):
    return lax.dot_general(a, b, COLS, preferred_element_type=F32)


def gelu_both(u):
    u2 = u * u
    t = jnp.tanh(GC * (u + 0.044715 * (u2 * u)))
    half = 0.5 * (1.0 + t)
    return u * half, half + (0.5 * u) * (1.0 - t * t) * (GC + (3.0 * 0.044715 * GC) * u2)


def loop(n, body):
    lax.fori_loop(0, n, lambda i, c: (body(i), c)[1], 0)


def local(src, dst, sem):
    return pltpu.make_async_copy(src, dst, sem)


def remote(src, dst, ss, rs, dev):
    return pltpu.make_async_remote_copy(src_ref=src, dst_ref=dst, send_sem=ss, recv_sem=rs, device_id=dev, device_id_type=MESH)


def kernel(dims, x, y, w1, w2, m1, r1, m2, r2, lb, ha, ea, ub, gb, qb, ua, ga, qa, vx, pb,
           lacc, z_s, z_r, d_s, d_r, v_s, v_r, n_s, n_r, x_s, x_r, f_s, f_r, h_s, h_r, ms_s, ms_r, pe_s, pe_r, ls_s, ls_r):
    nm, T, D, Fk, fs, inv = dims
    nj = Fk // fs
    nq = nj // 2
    nt = 2 * nm
    T2 = 2 * T
    dq, dr = D // 4, D // 8
    s = lax.axis_index('stage')
    r = lax.axis_index('data')
    k = r % 2
    xb = (r // 2) % 2
    yb_ = r // 4
    pr = r + 1 - 2 * k
    fx = r + 2 - 4 * xb
    fy = r + 4 - 8 * yb_
    dg = fy + 2 - 4 * xb
    ry, rx = fy - k, fx - k + 1
    nb = fy * (1 - k) + fx * k
    pe = fx * (1 - k) + fy * k
    fb = k * Fk
    fq = fb + (yb_ * (1 - k) + xb * k) * (Fk // 2)
    own = pl.ds(pl.multiple_of(k * T, T), T)
    oth = pl.ds(pl.multiple_of((1 - k) * T, T), T)
    is0, is1 = s == 0, s == 1

    def fcols(j):
        return pl.ds(pl.multiple_of(j * fs, fs), fs)

    def wcols(j, base):
        return pl.ds(pl.multiple_of(base + j * fs, fs), fs)

    def chip_cols(dev):
        return pl.ds(pl.multiple_of((dev // 2) * dq, 128), dq)

    def give(src, A, n, i, far):
        out = [
            remote(src, A.at[0, i, own], d_s.at[n], d_r.at[n], (s, pr)),
            remote(src, A.at[1, i, own], n_s.at[n, 0], n_r.at[n, k], (s, ry)),
            remote(src, A.at[1, i, own], n_s.at[n, 1], n_r.at[n, k], (s, rx)),
        ]
        if far:
            out.append(remote(src, A.at[3, i, own], x_s.at[n], x_r.at[n], (s, dg)))
        return out

    def got_half(sem):
        return remote(ha.at[0, 0, own], ha.at[0, 0, oth], x_s.at[0], sem, (s, pr))

    @pl.when(is0)
    def _():
        for i in range(nm):
            for c in give(x.at[i], ha, i, i, True):
                c.start()

    def phase1(wb1, wb2, ab, acc, uo, ui, go, tmp, yb, ob, wsem, alsem, usem, isem, gsem, psem, lsem, hsem):
        lacc[...] = jnp.zeros_like(lacc)

        def sched(t):
            mid = (t > 0) & (t < nt - 1)
            kind1 = jnp.where(mid, (t + 1) % 2, jnp.where(t == 0, 0, 1))
            i1 = jnp.where(mid, jnp.where(t % 2 == 1, (t + 1) // 2, (t - 2) // 2), jnp.where(t == 0, 0, nm - 1))
            return jnp.where(is1, kind1, 0), jnp.where(is1, i1, t)

        def c_w1(j):
            return local(w1.at[:, wcols(j, fb)], wb1.at[j % 2], wsem.at[0, j % 2])

        def c_w2(j):
            return local(w2.at[wcols(j, fb), :], wb2.at[j % 2], wsem.at[1, j % 2])

        def prep_a(t):
            kind, i = sched(t)

            @pl.when(is1 & (kind == 0))
            def _():
                got_half(z_r.at[i]).wait_recv()
                for c in give(ha.at[0, i, own], ha, i, i, False):
                    c.start()

        def u_in(i, j):
            return local(ub.at[i, :, fcols(j)], ui.at[j % 2], isem.at[j % 2])

        def prep_b(t):
            kind, i = sched(t)
            ap = t % 2
            for kk, A in ((0, ha), (1, ea)):
                @pl.when(kind == kk)
                def _():
                    got_half(d_r.at[kk * nm + i]).wait_recv()
                    if kk == 1:
                        local(ob.at[0], ea.at[0, i, own], lsem.at[i]).wait()
                        u_in(i, 0).start()
                    if kk == 0:
                        @pl.when(is0)
                        def _():
                            local(x.at[i], ab.at[ap, own], alsem.at[ap, 0]).start()

                    @pl.when(is1)
                    def _():
                        local(A.at[0, i, own], ab.at[ap, own], alsem.at[ap, 0]).start()
                    local(A.at[0, i, oth], ab.at[ap, oth], alsem.at[ap, 1]).start()

        def exchange(t):
            kind, i = sched(t)
            n = kind * nm + i
            return remote(acc.at[t % 2, oth], vx.at[n], v_s.at[n], v_r.at[n], (s, pr))

        def wait_out(t):
            kind, i = sched(t)

            @pl.when(is0 | (kind == 1))
            def _():
                n = kind * nm + i
                remote(ob.at[0], ea.at[0, i, own], z_s.at[n], z_r.at[n], (1 - s, r)).wait_send()

            @pl.when(is1 & (kind == 0))
            def _():
                for c in give(ob.at[0], ea, nm + i, i, False):
                    c.wait_send()

        def post_a(t):
            kind, i = sched(t)
            exchange(t).wait()
            local(vx.at[kind * nm + i], tmp, psem.at[0]).start()
            local(y.at[i], yb, psem.at[1]).start()

        def post_b(t):
            kind, i = sched(t)
            n = kind * nm + i
            ap = t % 2

            @pl.when(t >= 2)
            def _():
                wait_out(t - 2)
            local(vx.at[n], tmp, psem.at[0]).wait()
            local(y.at[i], yb, psem.at[1]).wait()
            last = is1 & (kind == 0)
            rb = min(64, T)

            def rows(b):
                lo = pl.ds(pl.multiple_of(b * rb, rb), rb)
                mine = pl.ds(pl.multiple_of(k * T + b * rb, rb), rb)
                h = (ab[ap, mine, :].astype(F32) + (acc[ap, mine, :] + tmp[lo, :])).astype(BF16)

                @pl.when(last)
                def _():
                    d = h.astype(F32) - yb[lo, :].astype(F32)
                    ob[ap, lo, :] = (d * inv).astype(BF16)
                    sq = jnp.sum((d * d).reshape(rb // 8, 8, D), axis=0)
                    part = lacc[...]
                    for c in range(D // 128):
                        part = part + sq[:, c * 128:(c + 1) * 128]
                    lacc[...] = part

                @pl.when(jnp.logical_not(last))
                def _():
                    ob[ap, lo, :] = h
            loop(T // rb, rows)

            @pl.when(is0)
            def _():
                remote(ob.at[ap], ha.at[0, i, own], z_s.at[n], z_r.at[n], (1 - s, r)).start()

            @pl.when(is1 & (kind == 1))
            def _():
                remote(ob.at[ap], ea.at[0, i, own], z_s.at[n], z_r.at[n], (1 - s, r)).start()

            @pl.when(last)
            def _():
                for c in give(ob.at[ap], ea, nm + i, i, False):
                    c.start()
                local(ob.at[ap], ea.at[0, i, own], lsem.at[i]).start()

        j_a = max(0, nj // 2 - 2)
        j_b = j_a + 1
        j_c = min(j_b + 1, nj - 2)
        j_d = nj - 2

        def slot(t):
            kind, i = sched(t)
            ap = t % 2
            more = t + 1 < nm + nm * s

            @pl.when(is0 | (t == 0))
            def _():
                prep_a(t)
                prep_b(t)

            local(ha.at[0, i, own], ab.at[ap, own], alsem.at[ap, 0]).wait()
            local(ha.at[0, i, oth], ab.at[ap, oth], alsem.at[ap, 1]).wait()

            @pl.when(is0)
            def _():
                local(ab.at[ap, own], ha.at[0, i, own], hsem).start()

            def hooks(j):
                late = is1 & (t > 0)

                @pl.when(late & (j == j_a))
                def _():
                    post_a(t - 1)

                @pl.when(late & (j == j_b))
                def _():
                    post_b(t - 1)

                @pl.when(is1 & more & (j == jnp.where(t == 0, j_d, j_c)))
                def _():
                    prep_a(t + 1)

                @pl.when(is1 & more & (j == j_d))
                def _():
                    prep_b(t + 1)

            def run(c1, c2, before, first, second, after):
                c1(0).wait()
                c1(1).start()
                before(0)
                acc[ap] = jnp.zeros((T2, D), F32)
                first(0)
                after(0)

                def step(j):
                    c1(j + 1).wait()
                    c2(j).wait()

                    @pl.when(j + 2 < nj)
                    def _():
                        c1(j + 2).start()
                    c2(j + 1).start()
                    hooks(j)
                    before(j + 1)
                    first(j + 1)
                    acc[ap] += second(j)
                    after(j + 1)
                loop(nj - 1, step)
                c2(nj - 1).wait()

                @pl.when(more)
                def _():
                    c_w1(0).start()
                    c_w2(0).start()
                acc[ap] += second(nj - 1)

            def g_out(j, dst):
                return local(go.at[j % 2], dst.at[i, :, fcols(j)], gsem.at[j % 2])

            def u_out(j):
                return local(uo.at[j % 2], ub.at[i, :, fcols(j)], usem.at[j % 2])

            @pl.when(kind == 0)
            def _():
                def before(j):
                    @pl.when(j >= 2)
                    def _():
                        u_out(j - 2).wait()
                        g_out(j - 2, gb).wait()

                def first(j):
                    for h in (slice(0, T), slice(T, T2)):
                        g, uo[j % 2, h] = gelu_both(dot(ab[ap, h], wb1[j % 2]))
                        go[j % 2, h] = g.astype(BF16)

                def after(j):
                    u_out(j).start()
                    g_out(j, gb).start()
                run(c_w1, c_w2, before, first, lambda j: dot(go[j % 2], wb2[j % 2]), after)
                for j in (nj - 2, nj - 1):
                    u_out(j).wait()
                    g_out(j, gb).wait()

            @pl.when(kind == 1)
            def _():
                def before(j):
                    @pl.when(j >= 2)
                    def _():
                        g_out(j - 2, qb).wait()
                    u_in(i, j).wait()

                    @pl.when(j + 1 < nj)
                    def _():
                        u_in(i, j + 1).start()

                def first(j):
                    p = dot_cols(ab[ap], wb2[j % 2]).astype(BF16)
                    go[j % 2] = (p.astype(F32) * ui[j % 2]).astype(BF16)
                run(c_w2, c_w1, before, first, lambda j: dot_cols(go[j % 2], wb1[j % 2]), lambda j: g_out(j, qb).start())
                for j in (nj - 2, nj - 1):
                    g_out(j, qb).wait()

            @pl.when(is0)
            def _():
                local(ab.at[ap, own], ha.at[0, i, own], hsem).wait()
            exchange(t).start()

            @pl.when(is0 | (t == nt - 1))
            def _():
                post_a(t)
                post_b(t)

        c_w1(0).start()
        c_w2(0).start()
        n_slots = nm + nm * s
        lax.fori_loop(0, n_slots, lambda t, c: (slot(t), c)[1], 0)
        wait_out(n_slots - 2)
        wait_out(n_slots - 1)

    pl.run_scoped(
        phase1,
        VMEM((2, D, fs), BF16), VMEM((2, fs, D), BF16), VMEM((2, T2, D), BF16), VMEM((2, T2, D), F32),
        VMEM((2, T2, fs), F32), VMEM((2, T2, fs), F32), VMEM((2, T2, fs), BF16),
        VMEM((T, D), F32), VMEM((T, D), BF16), VMEM((2, T, D), BF16),
        DMA((2, 2)), DMA((2, 2)), DMA((2,)), DMA((2,)), DMA((2,)), DMA((2,)), DMA((nm,)), DMA,
    )

    def loss_copy(d):
        return remote(lacc, lb.at[r], ls_s.at[d], ls_r.at[r], (d // 8, d % 8))

    def loss_self():
        return local(lacc, lb.at[r], ls_s.at[8 + r])

    @pl.when(is1)
    def _():
        def send(d):
            @pl.when(d != 8 + r)
            def _():
                loss_copy(d).start()
        loop(16, send)
        loss_self().start()

    nc = 4 * nm

    def all_tokens(wq1, wq2, ab, uo, ui, go, qsem, alsem, usem, isem, gsem):
        def c_q1(j):
            return local(w1.at[:, wcols(j, fq)], wq1.at[j], qsem.at[0, j])

        def c_q2(j):
            return local(w2.at[wcols(j, fq), :], wq2.at[j], qsem.at[1, j])
        for j in range(nq):
            c_q1(j).start()

        def arrive(A, n, c, i):
            @pl.when(c == 1)
            def _():
                for h in range(2):
                    got_half(n_r.at[n, h]).wait_recv()
                remote(A.at[1, i], A.at[2, i], f_s.at[n], f_r.at[n], (s, pr)).start()

            @pl.when(c == 2)
            def _():
                remote(A.at[1, i], A.at[2, i], f_s.at[n], f_r.at[n], (s, pr)).wait_recv()

            @pl.when(c == 3)
            def _():
                got_half(x_r.at[n]).wait_recv()
                remote(A.at[3, i, own], A.at[3, i, own], h_s.at[n], h_r.at[n], (s, pr)).start()
                got_half(h_r.at[n]).wait_recv()

        def c_ab(A, c, i, v):
            return local(A.at[c, i], ab.at[v % 2], alsem.at[v % 2])

        def block(c, i):
            return pl.ds(pl.multiple_of((c * nm + i) * T2, T2), T2)

        def run(A, at, ready, before, first, outs):
            def load(v):
                c, i = at(v)
                ready(c, i)
                c_ab(A, c, i, v).start()
            load(0)

            def chunk(v):
                c, i = at(v)
                c_ab(A, c, i, v).wait()

                def step(j):
                    g = v * nq + j

                    @pl.when((j == nq - 1) & (v + 1 < nc))
                    def _():
                        load(v + 1)

                    @pl.when(g >= 2)
                    def _():
                        for o in outs(g - 2):
                            o.wait()
                    before(g)
                    first(v, j, g % 2)
                    for o in outs(g):
                        o.start()
                loop(nq, step)
            loop(nc, chunk)
            for g in (nc * nq - 2, nc * nq - 1):
                for o in outs(g):
                    o.wait()

        def at_h(v):
            return v // nm, v % nm

        def outs_h(g):
            c, i = at_h(g // nq)
            return [local(uo.at[g % 2], ua.at[block(c, i), fcols(g % nq)], usem.at[g % 2]),
                    local(go.at[g % 2], ga.at[block(c, i), fcols(g % nq)], gsem.at[g % 2])]

        def before_h(g):
            @pl.when(g < nq)
            def _():
                c_q1(g).wait()
                c_q2(g).start()

        def first_h(v, j, sl):
            for h in (slice(0, T), slice(T, T2)):
                g, uo[sl, h] = gelu_both(dot(ab[v % 2, h], wq1[j]))
                go[sl, h] = g.astype(BF16)
        run(ha, at_h, lambda c, i: arrive(ha, i, c, i), before_h, first_h, outs_h)

        def at_e(v):
            return v % 4, v // 4

        def outs_e(g):
            c, i = at_e(g // nq)
            return [local(go.at[g % 2], qa.at[block(c, i), fcols(g % nq)], gsem.at[g % 2])]

        def u_in(g):
            c, i = at_e(g // nq)
            return local(ua.at[block(c, i), fcols(g % nq)], ui.at[g % 2], isem.at[g % 2])

        def before_e(g):
            @pl.when(g < nq)
            def _():
                c_q2(g).wait()
            u_in(g).wait()

            @pl.when(g + 1 < nc * nq)
            def _():
                u_in(g + 1).start()

        def ready_e(c, i):
            n = nm + i

            @pl.when(c == 0)
            def _():
                got_half(z_r.at[n]).wait_recv()
                for cp in give(ea.at[0, i, own], ea, n, i, True):
                    cp.start()
                got_half(d_r.at[n]).wait_recv()
            arrive(ea, n, c, i)

        def first_e(v, j, sl):
            p = dot_cols(ab[v % 2], wq2[j]).astype(BF16)
            go[sl] = (p.astype(F32) * ui[sl]).astype(BF16)
        u_in(0).start()
        run(ea, at_e, ready_e, before_e, first_e, outs_e)

    def sums0(hv, bv, o, tb, tsem, bsem, osem):
        nw = 4 * nq

        def at(w):
            return w // (2 * nq), (w // 2) % nq, w % 2

        def load(w):
            _, j, q = at(w)
            for qq, A in ((0, qa), (1, ga)):
                @pl.when(q == qq)
                def _():
                    local(A.at[:, fcols(j)], bv.at[w % 2], bsem.at[w % 2]).start()

        def far(w, q, m):
            j = at(w)[1]
            return remote(pb.at[q, j, 2 + m], (m1, m2)[q].at[:, wcols(j, fq)], pe_s.at[q, m, j], pe_r.at[q, k, j], (s, nb - k + m))

        def near(w, q):
            j = at(w)[1]
            return remote(pb.at[q, j, 1 - k], (m1, m2)[q].at[:, wcols(j, fq)], ms_s.at[q, j], ms_r.at[q, j], (s, pr))

        def ship(w):
            ps, j, q = at(w)
            for qq in range(2):
                @pl.when(q == qq)
                def _():
                    for m in range(2):
                        local(o.at[qq, m], pb.at[qq, j, m], osem.at[qq, m]).wait()

                    @pl.when(ps == 0)
                    def _():
                        for m in range(2):
                            far(w, qq, m).start()

                    @pl.when(ps == 1)
                    def _():
                        near(w, qq).start()

        def one(ps):
            cols = pl.ds(pl.multiple_of((nb // 2) * dq * (1 - ps) + (r // 2) * dq * ps, 128), dq)
            for qq, A in ((0, ha), (1, ea)):
                def c_t(v):
                    return local(A.at[v // nm, v % nm, :, cols], tb.at[v % 2], tsem.at[v % 2])
                c_t(0).start()

                def build(v):
                    c_t(v).wait()

                    @pl.when(v + 1 < nc)
                    def _():
                        c_t(v + 1).start()
                    hv[qq, :, pl.ds(pl.multiple_of(v * T2, T2), T2)] = tb[v % 2].T
                loop(nc, build)

            def unit(ww):
                w = ps * 2 * nq + ww
                _, j, q = at(w)
                local(qa.at[:, fcols(j)], bv.at[w % 2], bsem.at[w % 2]).wait()

                @pl.when(w + 1 < nw)
                def _():
                    load(w + 1)

                @pl.when(w >= 1)
                def _():
                    ship(w - 1)

                def grads(m):
                    rows = pl.ds(pl.multiple_of(m * dr, dr), dr)
                    o[q, m] = dot(hv[q, rows, :], bv[w % 2])
                    for qq, M in ((0, m1), (1, m2)):
                        here = (ps == 1) & (m == k)

                        @pl.when((q == qq) & here)
                        def _():
                            local(o.at[qq, m], M.at[:, wcols(j, fq)], osem.at[qq, m]).start()

                        @pl.when((q == qq) & jnp.logical_not(here))
                        def _():
                            local(o.at[qq, m], pb.at[qq, j, 2 * (1 - ps) + m], osem.at[qq, m]).start()
                loop(2, grads)
            loop(2 * nq, unit)
        load(0)
        loop(2, one)
        ship(nw - 1)

        def finish(j):
            w = 2 * j
            for q in range(2):
                near(w, q).wait()
                for m in range(2):
                    far(w, q, m).wait_send()
                    remote(pb.at[q, j, 0], (m1, m2)[q].at[:, wcols(j, fq)], ms_s.at[q, j], pe_r.at[q, m, j], (s, pr)).wait_recv()
        loop(nq, finish)

    def sums1(wb1, wb2, ht, et, gv, qv, a, b, o, tb, dv, wsem, tsem, asem, gqsem, osem):
        def weights(j):
            return (local(w1.at[:, wcols(j, fb)], wb1.at[j % 2], wsem.at[0, j % 2]),
                    local(w2.at[wcols(j, fb), :], wb2.at[j % 2], wsem.at[1, j % 2]))

        def stream(v):
            i, sl = v % nm, v % 2
            return (local(ha.at[1, i], a.at[sl], asem.at[0, sl]), local(ea.at[1, i], b.at[sl], asem.at[1, sl]))

        def saved(j, i):
            rows = pl.ds(pl.multiple_of(i * T2, T2), T2)
            return (local(gb.at[i, :, fcols(j)], gv.at[rows], gqsem.at[0, i]),
                    local(qb.at[i, :, fcols(j)], qv.at[rows], gqsem.at[1, i]))

        for c in weights(0):
            c.start()

        cols = (chip_cols(r), chip_cols(pe))
        for q, A, dst in ((0, ha, ht), (1, ea, et)):
            def c_t(v):
                return [local(A.at[v // nm, v % nm, :, cols[c]], tb.at[v % 2, c], tsem.at[v % 2, c]) for c in range(2)]

            def start(v):
                @pl.when(v >= nm)
                def _():
                    for h in range(2):
                        got_half(n_r.at[q * nm + v - nm, h]).wait_recv()
                for c in c_t(v):
                    c.start()
            start(0)

            def build(v):
                for c in c_t(v):
                    c.wait()

                @pl.when(v + 1 < 2 * nm)
                def _():
                    start(v + 1)
                for c in range(2):
                    dst[c * dq:(c + 1) * dq, pl.ds(pl.multiple_of(v * T2, T2), T2)] = tb[v % 2, c].T
            loop(2 * nm, build)

        for c in stream(0):
            c.start()

        def kept(q, j, m):
            mine = local(o.at[q, m], (m1, m2)[q].at[:, wcols(j, fb)], osem.at[q, m])
            rest = local(o.at[q, m], pb.at[q, j, m], osem.at[q, m])
            return mine, rest

        def sends(j):
            cs = wcols(j, fb)
            out = []
            for q in range(2):
                for c in range(2):
                    out.append(remote(pb.at[q, j, 2 + c], (r1, r2)[q].at[:, cs], pe_s.at[q, c, j], pe_r.at[q, k, j], (s, pe - k + c)))
                out.append(remote(pb.at[q, j, 1 - k], (m1, m2)[q].at[:, cs], ms_s.at[q, j], ms_r.at[q, j], (s, pr)))
            return out

        def ship(j):
            for q in range(2):
                loop(4, lambda m: kept(q, j, m)[1].wait())
            for c in sends(j):
                c.start()

        def part(j):
            ws = j % 2
            loop(nm, lambda i: [c.start() for c in saved(j, i)])
            for c in weights(j):
                c.wait()

            @pl.when(j + 1 < nj)
            def _():
                for c in weights(j + 1):
                    c.start()

            @pl.when(j >= 1)
            def _():
                ship(j - 1)

            def again(i):
                v = j * nm + i
                sl = v % 2
                for c in stream(v):
                    c.wait()

                @pl.when(v + 1 < nj * nm)
                def _():
                    for c in stream(v + 1):
                        c.start()
                rows = pl.ds(pl.multiple_of((nm + i) * T2, T2), T2)
                for h in range(2):
                    part_rows = pl.ds(pl.multiple_of((nm + i) * T2 + h * T, T), T)
                    g, dv[h * T:(h + 1) * T] = gelu_both(dot(a[sl, h * T:(h + 1) * T], wb1[ws]))
                    gv[part_rows, :] = g.astype(BF16)
                p = dot_cols(b[sl], wb2[ws]).astype(BF16)
                qv[rows, :] = (p.astype(F32) * dv[...]).astype(BF16)
            loop(nm, again)
            loop(nm, lambda i: [c.wait() for c in saved(j, i)])

            def grads(m):
                rows = pl.ds(pl.multiple_of(m * dr, dr), dr)
                o[0, m] = dot(ht[rows, :], qv[...])
                o[1, m] = dot(et[rows, :], gv[...])
                for q in range(2):
                    mine, rest = kept(q, j, m)

                    @pl.when(m == k)
                    def _():
                        mine.start()

                    @pl.when(m != k)
                    def _():
                        rest.start()
            loop(4, grads)
        loop(nj, part)
        ship(nj - 1)

        def finish(j):
            for c in sends(j):
                c.wait_send()
            for q in range(2):
                remote(pb.at[q, j, 0], (m1, m2)[q].at[:, wcols(j, fb)], ms_s.at[q, j], ms_r.at[q, j], (s, pr)).wait_recv()
                for c in range(2):
                    remote(pb.at[q, j, 0], (r1, r2)[q].at[:, wcols(j, fb)], ms_s.at[q, j], pe_r.at[q, c, j], (s, pr)).wait_recv()
        loop(nj, finish)

    nr = 2 * nm * T2

    @pl.when(is0)
    def _():
        pl.run_scoped(
            all_tokens,
            VMEM((nq, D, fs), BF16), VMEM((nq, fs, D), BF16), VMEM((2, T2, D), BF16),
            VMEM((2, T2, fs), F32), VMEM((2, T2, fs), F32), VMEM((2, T2, fs), BF16),
            DMA((2, nq)), DMA((2,)), DMA((2,)), DMA((2,)), DMA((2,)),
        )
        pl.run_scoped(
            sums0,
            VMEM((2, dq, 2 * nr), BF16), VMEM((2, 2 * nr, fs), BF16), VMEM((2, 2, dr, fs), F32), VMEM((2, T2, dq), BF16),
            DMA((2,)), DMA((2,)), DMA((2, 2)),
        )

    @pl.when(is1)
    def _():
        pl.run_scoped(
            sums1,
            VMEM((2, D, fs), BF16), VMEM((2, fs, D), BF16),
            VMEM((2 * dq, nr), BF16), VMEM((2 * dq, nr), BF16), VMEM((nr, fs), BF16), VMEM((nr, fs), BF16),
            VMEM((2, T2, D), BF16), VMEM((2, T2, D), BF16), VMEM((2, 4, dr, fs), F32), VMEM((2, 2, T2, dq), BF16), VMEM((T2, fs), F32),
            DMA((2, 2)), DMA((2, 2)), DMA((2, 2)), DMA((2, nm)), DMA((2, 4)),
        )

    def settle(n):
        A = ha

        @pl.when(is0 | (n < nm))
        def _():
            for c in give(A.at[0, 0, own], A, n, 0, False):
                c.wait_send()

        @pl.when(is0)
        def _():
            remote(A.at[3, 0, own], A.at[3, 0, own], x_s.at[n], x_r.at[n], (s, dg)).wait_send()
            remote(A.at[3, 0, own], A.at[3, 0, own], h_s.at[n], h_r.at[n], (s, pr)).wait_send()
            remote(A.at[1, 0], A.at[2, 0], f_s.at[n], f_r.at[n], (s, pr)).wait_send()
    loop(nt, settle)

    @pl.when(is1)
    def _():
        def sent(d):
            @pl.when(d != 8 + r)
            def _():
                loss_copy(d).wait_send()
        loop(16, sent)
        loss_self().wait()

    def got(n):
        @pl.when(is0 | (n != r))
        def _():
            remote(lacc, lb.at[n], ls_s.at[n], ls_r.at[n], (s, r)).wait_recv()
    loop(8, got)


def solution(mesh):
    n_data = mesh.shape['data']

    def per_device(inputs, targets, w_up, w_down):
        nm, T, D = inputs.shape
        F = w_up.shape[2]
        Fk = F // 2
        fs = min(512, Fk // 4)
        nj = Fk // fs
        dr = D // 8
        inv = 1.0 / (n_data * nm * T)
        dims = (nm, T, D, Fk, fs, inv)
        sd = jax.ShapeDtypeStruct
        rows = 4 * nm * 2 * T
        out_shape = [
            sd((dr, F), F32), sd((dr, F), F32), sd((dr, F), F32), sd((dr, F), F32), sd((8, 8, 128), F32),
            sd((4, nm, 2 * T, D), BF16), sd((4, nm, 2 * T, D), BF16),
            sd((nm, 2 * T, Fk), F32), sd((nm, 2 * T, Fk), BF16), sd((nm, 2 * T, Fk), BF16),
            sd((rows, Fk // 2), F32), sd((rows, Fk // 2), BF16), sd((rows, Fk // 2), BF16),
            sd((2 * nm, T, D), F32), sd((2, nj, 4, dr, fs), F32),
        ]
        any_spec = pl.BlockSpec(memory_space=pl.ANY)
        n2 = 2 * nm
        outs = pl.pallas_call(
            functools.partial(kernel, dims),
            out_shape=out_shape,
            in_specs=[any_spec] * 4,
            out_specs=[any_spec] * len(out_shape),
            scratch_shapes=[
                VMEM((8, 128), F32),
                DMA((n2,)), DMA((n2,)), DMA((n2,)), DMA((n2,)), DMA((n2,)), DMA((n2,)), DMA((n2, 2)), DMA((n2, 2)),
                DMA((n2,)), DMA((n2,)), DMA((n2,)), DMA((n2,)), DMA((n2,)), DMA((n2,)),
                DMA((2, nj)), DMA((2, nj)), DMA((2, 2, nj)), DMA((2, 2, nj)), DMA((16,)), DMA((8,)),
            ],
            compiler_params=pltpu.CompilerParams(has_side_effects=True, vmem_limit_bytes=67_000_000),
            cost_estimate=pl.CostEstimate(flops=16 * nm * T * D * F, bytes_accessed=10**9, transcendentals=0),
            name='train_step',
        )(inputs, targets, w_up.reshape(D, F), w_down.reshape(F, D))
        m1, r1, m2, r2, lb = outs[:5]
        loss = jnp.sum(lb) * (0.5 * inv)
        whole = lax.axis_index('stage') == 0
        up = jnp.where(whole, m1, m1 + r1)
        down = jnp.where(whole, m2, m2 + r2)
        return loss, up[None], down.T[None]

    return jax.shard_map(per_device, mesh=mesh, in_specs=(P('data', None, None), P('data', None, None), P('stage', None, None), P('stage', None, None)), out_specs=(P(), P('stage', 'data', None), P('stage', None, 'data')), check_vma=False)
```

time: 880 us -> 1020 us (1.16)
  the two profiles are of different devices: /device:TPU:0 before, /device:TPU:3 now
where the time goes in v2:
time: 1020 us
  Pallas kernels  988 us (97%)
  other arithmetic  27.6 us (3%)
    pallas_call x1, Pallas kernels, per_device(): pl.pallas_call(functools.partial(kernel, dims), out_shape=out_shape, in_s...  988 us
    broadcast_in_dim x1, other arithmetic, per_device(): return (loss, up[None], down.T[None])  27 us

profile of v2, /device:TPU:3, one launch (start us, length us, event | category | flops | bytes accessed | tf_op | source)
XLA Modules:
  0.0 1018.1 jit_solution(13540346769617097025)
XLA Ops:
  0.6 988.0 %train_step.1 = (f32[320,10240]{1,0:T(8,128)}, f32[320,10240]{1,0:T(8,128)}, f32[320,10240]{1,0:T(8,128)}, f32[320,10240]{1,0:T(8,128)}, f32[8,8,128]{2,1,0:T(8,...) custom-call(bf16[4,256,2560]{2,1,0:T(8,128)(2,1)} %x.1, ...), custom_call_target="tpu_custom_call" | custom-call | flops 429496729600 | bytes 1000000000 | tf_op jit(solution)/shard_map/train_step/pallas_call | solution.py:802
  988.7 0.0 copy-start
  988.7 27.0 %fusion = (f32[1,320,10240]{2,1,0:T(8,128)}, f32[1,10240,320]{1,2,0:T(8,128)}) fusion(f32[320,10240]{1,0:T(8,128)} %get-tuple-element.9, f32[320,10240]{1,0:T(8,128)} %get-tuple-element.10, pred[]{:T(512)S(6)} %eq.3, f32[320,10240]{1,0:T(8,128)} %get-tuple-element.11, f32[320,10240]{1,0:T(8,128)} %get-tuple-element.12), kind=kLoop, calls=%fused_computation.2 | loop fusion | flops 13107200 | bytes 78643200 | tf_op jit(solution)/shard_map/broadcast_in_dim | solution.py:822
  1015.7 0.0 copy-done
  1015.7 0.6 reduce_sum.9
Async XLA Ops:
  988.7 27.0 %copy-start = (f32[8,8,128]{2,1,0:T(8,128)S(1)}, f32[8,8,128]{2,1,0:T(8,128)}, u32[]{:S(2)}) copy-start(f32[8,8,128]{2,1,0:T(8,128)} %get-tuple-element.8) | copy-start | bytes 98308
